TPU v7x, 32 devices: a whole 2x2x4 slice. The times are simulated.
32 devices in a mesh: sec: 4 (over y, core), op: 8 (over z, x).
Axes of the slice: x: 2, y: 2, z: 4, core: 2. Of those that a mesh axis runs over, the one named last changes fastest.
Arguments:
- wavefunction: bfloat16 [4, 512, 1024], P('sec', 'op'), may hold values from -4.5 to 4.5
- op_blocks: bfloat16 [8, 4, 1024, 1024], P('op', 'sec'), may hold values from -6 to 6
- basis_guess: bfloat16 [4, 1024, 512], P('sec'), may hold values from -4.5 to 4.5
- sector_sizes: int32 [4], replicated, may hold values from 768 to 1024
- kept_counts: int32 [4], replicated, may hold values from 256 to 512
- target_map: int32 [8, 4], replicated, may hold values from 0 to 3, as said below
- noise_numerator: int32 [1], replicated, may hold values from 256 to 1024
- noise_denominator: int32 [1], replicated, may hold values from 4194304 to 8388608
Outputs:
- kept_basis: float32 [4, 1024, 512], P('sec', 'op')
- rotated: float32 [8, 4, 512, 512], P('op', 'sec')
Inputs may be any that keep to these rules, and one draw needn't show every extreme that they name: For every operator k, target_map[k] is a permutation of the 4 sectors.
All inputs are finite; a program needn't handle non-finite values.
Results may differ from a plain program's by a relative error of at most 0.005.
Values may be sent and summed in bfloat16 or wider, within the bound.
A program may use at most 64 MiB of HBM per device.

v0:
```python
import jax
import jax.numpy as jnp
from jax import lax
from jax.sharding import PartitionSpec as P


def source_sectors(target_map):
    sectors = jnp.arange(target_map.shape[1], dtype=jnp.int32)
    matches = target_map[:, :, None] == sectors[None, None, :]
    return jnp.sum(jnp.where(matches, sectors[None, :, None], 0), axis=1)


def fetch_pieces(own_slice, wanted_all):
    everyone = lax.all_gather(own_slice, "sec", axis=0, tiled=True)
    outgoing = jnp.take(everyone, wanted_all, axis=0)
    incoming = lax.all_to_all(outgoing, "op", split_axis=1, concat_axis=1, tiled=True)
    return incoming.reshape(
        incoming.shape[0], incoming.shape[1] * incoming.shape[2], incoming.shape[3]
    )


def body(
    wavefunction,
    op_blocks,
    basis_guess,
    sector_sizes,
    kept_counts,
    target_map,
    noise_numerator,
    noise_denominator,
):
    highest = lax.Precision.HIGHEST
    local_count = wavefunction.shape[0]
    state_count = wavefunction.shape[2]
    kept_width = basis_guess.shape[2]
    tile_rows = state_count // lax.axis_size("op")
    sec_index = lax.axis_index("sec")
    op_index = lax.axis_index("op")
    noise_weight = noise_numerator[0].astype(jnp.float32) / noise_denominator[0].astype(jnp.float32)
    sources = source_sectors(target_map)
    own_sectors = sec_index * local_count + jnp.arange(local_count, dtype=jnp.int32)
    wanted_all = jnp.take(sources, own_sectors, axis=1).T
    wanted = lax.dynamic_index_in_dim(wanted_all, op_index, 1, keepdims=False)
    states = jnp.arange(state_count, dtype=jnp.int32)
    own_sizes = jnp.take(sector_sizes, own_sectors)
    own_mask = states[None, :] < own_sizes[:, None]
    source_mask = states[None, :] < jnp.take(sector_sizes, wanted)[:, None]
    own_kept = (
        jnp.arange(kept_width, dtype=jnp.int32)[None, :]
        < jnp.take(kept_counts, own_sectors)[:, None]
    )
    zero_half = jnp.zeros((), jnp.bfloat16)
    own_rows = jnp.where(own_mask[:, None, :], wavefunction, zero_half)
    moved = fetch_pieces(wavefunction, wanted_all)
    moved = jnp.where(source_mask[:, None, :], moved, zero_half)
    blocks = op_blocks[0]
    perturbed = jnp.einsum(
        "lcx,lxy->lcy", moved, blocks, preferred_element_type=jnp.float32
    ).astype(jnp.bfloat16)
    guess_rows = jnp.where(own_mask[:, :, None], basis_guess, zero_half)
    density_part = jnp.einsum(
        "lcx,lcy->lxy", own_rows, own_rows, preferred_element_type=jnp.float32
    )
    density_part = density_part + noise_weight * jnp.einsum(
        "lcx,lcy->lxy", perturbed, perturbed, preferred_element_type=jnp.float32
    )
    density_tile = lax.psum_scatter(density_part, "op", scatter_dimension=1, tiled=True)
    image = jnp.einsum(
        "lrx,lxk->lrk", density_tile, guess_rows.astype(jnp.float32), precision=highest
    )
    row_ids = op_index * tile_rows + jnp.arange(tile_rows, dtype=jnp.int32)
    row_mask = row_ids[None, :] < own_sizes[:, None]
    image = jnp.where(row_mask[:, :, None] & own_kept[:, None, :], image, jnp.float32(0.0))
    full_image = lax.all_gather(image, "op", axis=1, tiled=True)
    padding = jnp.where(own_kept, jnp.float32(0.0), jnp.float32(1.0))
    correlation = (
        jnp.einsum("ldk,ldm->lkm", full_image, full_image, precision=highest)
        + padding[:, :, None] * jnp.eye(kept_width, dtype=jnp.float32)[None]
    )
    factor = jnp.linalg.cholesky(correlation)
    new_basis = lax.linalg.triangular_solve(
        factor, full_image, left_side=False, lower=True, transpose_a=True
    )
    kept_tile = (
        lax.dynamic_slice_in_dim(new_basis, op_index * tile_rows, tile_rows, 1)
        * float(state_count) ** 0.5
    )
    basis_half = new_basis.astype(jnp.bfloat16)
    mapped = jnp.einsum(
        "lxy,lyk->lxk", blocks, basis_half, preferred_element_type=jnp.float32
    ).astype(jnp.bfloat16)
    own_tile = lax.dynamic_slice_in_dim(basis_half, op_index * tile_rows, tile_rows, 1)
    source_basis = fetch_pieces(own_tile, wanted_all)
    rotated = jnp.einsum("lxk,lxm->lkm", source_basis, mapped, preferred_element_type=jnp.float32)
    return (kept_tile, rotated[None])


def solution(mesh):
    placed = (
        P("sec", "op", None),
        P("op", "sec", None, None),
        P("sec", None, None),
        P(),
        P(),
        P(),
        P(),
        P(),
    )
    return jax.shard_map(
        body,
        mesh=mesh,
        in_specs=placed,
        out_specs=(P("sec", "op", None), P("op", "sec", None, None)),
        check_vma=False,
    )
```

profile of v0, /device:TPU:0, one launch (start us, length us, event | category | flops | bytes accessed | tf_op | source)
XLA Modules:
  0.0 423.8 jit_solution(12136602973328848406)
XLA Ops:
  8.1 8.9 %all_gather.9 = bf16[4,64,1024]{2,1,0:T(8,128)(2,1)S(1)} all-gather(bf16[1,64,1024]{2,1,0:T(8,128)(2,1)} %param.8), channel_id=1, replica_groups=mesh['sec'=4,'op'=8] {'sec'}, dimensions={0}, use_global_device_ids=true | all-gather | bytes 655360 | tf_op jit(solution)/shard_map/all_gather | solution.py:14
  17.0 1.6 gather_fusion
  18.5 2.4 fusion.38
  20.9 5.8 %all-to-all-start = ((bf16[1,8,64,1024]{3,2,0,1:T(8,128)(2,1)}), bf16[1,8,64,1024]{3,2,0,1:T(8,128)(2,1)S(1)}, u32[]{:S(2)}, u32[]{:S(2)}) async-start(bf16[1,8,64,1024]{3,2,0,1:T(8,128)(2,1)} %fusion.38), calls=%async_computation | async-start | bytes 2097152 | tf_op jit(solution)/shard_map/all_to_all | solution.py:16
  32.5 2.7 fusion.51
  35.1 17.9 %all-to-all-done = bf16[1,8,64,1024]{3,2,0,1:T(8,128)(2,1)S(1)} async-done(((bf16[1,8,64,1024]{3,2,0,1:T(8,128)(2,1)}), bf16[1,8,64,1024]{3,2,0,1:T(8,128)(2,1)S(1)}, u32[]{:S(2)}, u32[]{:S(2)}) %all-to-all-start) | async-done | bytes 1048608 | tf_op jit(solution)/shard_map/all_to_all | solution.py:16
  54.1 8.2 %add_bitcast_fusion = f32[1,1024,1024]{2,1,0:T(8,128)} fusion(f32[1024,1024]{1,0:T(8,128)} %fusion.51, f32[]{:T(128)} %bitcast.5, bf16[512,1024]{1,0:T(8,128)(2,1)} %bitcast.230, bf16[1,1,1024,1024]{3,2,1,0:T(8,128)(2,1)S(1)} %copy-done), kind=kOutput, calls=%fused_computation.4 | convolution fusion | flops 2150105088 | bytes 11534340 | tf_op jit(solution)/shard_map/lcx,lcy->lxy/dot_general | solution.py:64
  64.2 85.2 %reduce-scatter.2.cloned.1.call-done = f32[1,128,1024]{2,1,0:T(8,128)} async-done(((f32[1,1024,1024]{2,1,0:T(8,128)}), f32[1,128,1024]{2,1,0:T(8,128)}) %reduce-scatter.2.cloned.1.call-update) | async-done | bytes 524304 | tf_op jit(solution)/shard_map/reduce_scatter | solution.py:67
  149.4 2.4 convolution_select_fusion
  151.9 49.0 %all-gather.3.cloned.1.call-done = f32[1024,512]{1,0:T(8,128)} async-done(((f32[128,512]{1,0:T(8,128)}), f32[1024,512]{1,0:T(8,128)}) %all-gather.3.cloned.1.call-update) | async-done | bytes 2097168 | tf_op jit(solution)/shard_map/all_gather | solution.py:74
  200.9 5.7 %convolution_add_fusion = f32[512,512]{0,1:T(8,128)S(1)} fusion(f32[1024,512]{1,0:T(8,128)} %all-gather.3.cloned.1.call-done, f32[512]{0:T(512)S(1)} %broadcast_select_fusion.1), kind=kOutput, calls=%fused_computation.19 | convolution fusion | flops 3222011904 | bytes 3147776 | tf_op jit(solution)/shard_map/ldk,ldm->lkm/dot_general | solution.py:77
  210.4 11.7 %custom-call.34 = f32[1,128,128]{2,1,0:T(8,128)S(1)} custom-call(f32[1,128,128]{2,1,0:T(8,128)S(1)} %cholesky.267), custom_call_target="Cholesky" | custom-call | tf_op jit(solution)/shard_map/jit(cholesky)/cholesky | solution.py:80
  222.1 9.8 %custom-call.35 = f32[1,1,128,128]{2,3,1,0:T(8,128)S(1)} custom-call(f32[1,1,128,128]{3,2,1,0:T(8,128)S(1)} %get-tuple-element.83), custom_call_target="InvertDiagBlocksLowerTriangular" | custom-call | tf_op jit(solution)/shard_map/jit(cholesky)/cholesky | solution.py:80
  234.6 11.9 %custom-call.36 = f32[1,128,128]{2,1,0:T(8,128)S(1)} custom-call(f32[1,128,128]{2,1,0:T(8,128)S(1)} %cholesky.271), custom_call_target="Cholesky" | custom-call | tf_op jit(solution)/shard_map/jit(cholesky)/cholesky | solution.py:80
  246.5 9.8 %custom-call.37 = f32[1,1,128,128]{2,3,1,0:T(8,128)S(1)} custom-call(f32[1,1,128,128]{3,2,1,0:T(8,128)S(1)} %get-tuple-element.80), custom_call_target="InvertDiagBlocksLowerTriangular" | custom-call | tf_op jit(solution)/shard_map/jit(cholesky)/cholesky | solution.py:80
  257.9 11.7 %custom-call.38 = f32[1,128,128]{2,1,0:T(8,128)S(1)} custom-call(f32[1,128,128]{2,1,0:T(8,128)S(1)} %cholesky.276), custom_call_target="Cholesky" | custom-call | tf_op jit(solution)/shard_map/jit(cholesky)/cholesky | solution.py:80
  270.4 9.8 %custom-call.39 = f32[1,1,128,128]{2,3,1,0:T(8,128)S(1)} custom-call(f32[1,1,128,128]{3,2,1,0:T(8,128)S(1)} %get-tuple-element.77), custom_call_target="InvertDiagBlocksLowerTriangular" | custom-call | tf_op jit(solution)/shard_map/jit(cholesky)/cholesky | solution.py:80
  281.6 11.7 %custom-call.40 = f32[1,128,128]{2,1,0:T(8,128)S(1)} custom-call(f32[1,128,128]{2,1,0:T(8,128)S(1)} %fusion.26), custom_call_target="Cholesky" | custom-call | tf_op jit(solution)/shard_map/jit(cholesky)/cholesky | solution.py:80
  298.3 14.5 %while.5 = (s32[]{:T(128)}, f32[1,512,512]{2,1,0:T(8,128)}, s32[4,2]{0,1:T(2,128)S(1)}, f32[4,1,128,128]{3,2,1,0:T(8,128)}, s32[]{:T(128)}) while((s32[]{:T(128)}, f32[1,512,512]{2,1,0:T(8,128)}, s32[4,2]{0,1:T(2,128)S(1)}, f32[4,1,128,128]{3,2,1,0:T(8,128)}, s32[]{:T(128)}) %tuple.61), condition=%wide.while_cond.4, body=%wide.while_body.4.sunk | while | flops 2 | bytes 132205 | solution.py:81
  299.1 2.9 bitcast_dynamic-update-slice_fusion.2
  302.7 2.9 bitcast_dynamic-update-slice_fusion.2
  306.3 2.9 bitcast_dynamic-update-slice_fusion.2
  309.9 2.9 bitcast_dynamic-update-slice_fusion.2
  312.8 40.1 %custom-call.41 = f32[1,4,128,128]{2,3,1,0:T(8,128)S(1)} custom-call(f32[1,4,128,128]{3,2,1,0:T(8,128)} %bitcast.231), custom_call_target="InvertDiagBlocksLowerTriangular" | custom-call | tf_op jit(solution)/shard_map/triangular_solve | solution.py:81
  352.9 2.5 fusion.74
  355.5 2.1 fusion.17
  358.9 2.7 fusion.21
  363.0 3.7 fusion.19
  369.7 7.1 %all_gather.11 = bf16[4,128,512]{2,1,0:T(8,128)(2,1)S(1)} all-gather(bf16[1,128,512]{2,1,0:T(8,128)(2,1)S(1)} %copy.30), channel_id=1, replica_groups=mesh['sec'=4,'op'=8] {'sec'}, dimensions={0}, use_global_device_ids=true | all-gather | bytes 655360 | tf_op jit(solution)/shard_map/all_gather | solution.py:14
  381.2 3.6 all-to-all-start.1
  386.6 24.7 %all-to-all-done.1 = bf16[1,8,128,512]{2,3,0,1:T(8,128)(2,1)S(1)} async-done(((bf16[1,8,128,512]{2,3,0,1:T(8,128)(2,1)}), bf16[1,8,128,512]{2,3,0,1:T(8,128)(2,1)S(1)}, u32[]{:S(2)}, u32[]{:S(2)}) %all-to-all-start.1) | async-done | bytes 1048608 | tf_op jit(solution)/shard_map/all_to_all | solution.py:16
  412.5 4.2 convolution_bitcast_fusion
  (78 shorter events, 32.8 us)
Async XLA Ops:
  7.2 46.9 %copy-start = (bf16[1,1,1024,1024]{3,2,1,0:T(8,128)(2,1)S(1)}, bf16[1,1,1024,1024]{3,2,1,0:T(8,128)(2,1)}, u32[]{:S(2)}) copy-start(bf16[1,1,1024,1024]{3,2,1,0:T(8,128)(2,1)} %param.9) | copy-start | bytes 6291460
  18.5 12.0 %copy-start.6 = (s32[4]{0:T(128)S(1)}, s32[4]{0:T(128)}, u32[]{:S(2)}) copy-start(s32[4]{0:T(128)} %param.11) | copy-start | bytes 52
  18.5 13.9 %copy-start.4 = (bf16[1,64,1024]{2,1,0:T(8,128)(2,1)S(1)}, bf16[1,64,1024]{2,1,0:T(8,128)(2,1)}, u32[]{:S(2)}) copy-start(bf16[1,64,1024]{2,1,0:T(8,128)(2,1)} %param.8) | copy-start | bytes 393220
  20.9 32.1 %all-to-all-start = ((bf16[1,8,64,1024]{3,2,0,1:T(8,128)(2,1)}), bf16[1,8,64,1024]{3,2,0,1:T(8,128)(2,1)S(1)}, u32[]{:S(2)}, u32[]{:S(2)}) async-start(bf16[1,8,64,1024]{3,2,0,1:T(8,128)(2,1)} %fusion.38), calls=%async_computation | async-start | bytes 2097152 | tf_op jit(solution)/shard_map/all_to_all | solution.py:16
  26.7 122.7 %reduce-scatter.2.cloned.1.call-start = ((), (), s32[]{:S(2)}) async-start(), calls=%async_computation.3 | async-start | bytes 4718592 | tf_op jit(solution)/shard_map/reduce_scatter | solution.py:67
  62.3 0.7 copy-start.8
  62.3 87.2 %copy-start.7 = (bf16[1,1024,512]{2,1,0:T(8,128)(2,1)S(1)}, bf16[1,1024,512]{2,1,0:T(8,128)(2,1)}, u32[]{:S(2)}) copy-start(bf16[1,1024,512]{2,1,0:T(8,128)(2,1)} %param.10) | copy-start | bytes 3145732
  62.3 138.6 %all-gather.3.cloned.1.call-start = ((), (), s32[]{:S(2)}) async-start(), calls=%async_computation.4 | async-start | bytes 2359296 | tf_op jit(solution)/shard_map/all_gather | solution.py:74
  209.4 1.0 copy-start.3
  352.9 6.0 %copy-start.1 = (f32[1024,512]{1,0:T(8,128)S(1)}, f32[1024,512]{1,0:T(8,128)}, u32[]{:S(2)}) copy-start(f32[1024,512]{1,0:T(8,128)} %all-gather.3.cloned.1.call-done) | copy-start | bytes 6291460
  368.2 1.3 copy-start.2
  381.2 30.0 %all-to-all-start.1 = ((bf16[1,8,128,512]{2,3,0,1:T(8,128)(2,1)}), bf16[1,8,128,512]{2,3,0,1:T(8,128)(2,1)S(1)}, u32[]{:S(2)}, u32[]{:S(2)}) async-start(bf16[1,8,128,512]{2,3,0,1:T(8,128)(2,1)} %copy.31), calls=%async_computation.2 | async-start | bytes 2097152 | tf_op jit(solution)/shard_map/all_to_all | solution.py:16
  386.6 26.0 %copy-start.5 = (bf16[1024,128]{0,1:T(8,128)(2,1)S(1)}, bf16[1024,128]{0,1:T(8,128)(2,1)}, u32[]{:S(2)}) copy-start(bf16[1024,128]{0,1:T(8,128)(2,1)} %get-tuple-element.94) | copy-start | bytes 786436
Sparse Core Ops, SparseCore 0:
  62.4 86.9 reduce-scatter.1
  152.1 48.7 all-gather.2
where the time goes:
time: 429 us; the launch traced here: 424 us
  waiting for transfers between devices  177 us (41%)
  other arithmetic  128 us (30%)
  matrix products  43.8 us (10%)
  local copies, waits for them, and re-layouts  26.8 us (6%)
  between operations  22.2 us (5%)
  blocking collectives  16 us (4%)
  starting transfers between devices  9.91 us (2%)
    reduce_scatter x1, waiting for transfers between devices, body(): lax.psum_scatter(density_part, 'op', scatter_dimension=1, tiled=True)  85.2 us
    another operation x14, other arithmetic, body(): factor = jnp.linalg.cholesky(correlation)  78.6 us
    all_gather x1, waiting for transfers between devices, body(): full_image = lax.all_gather(image, 'op', axis=1, tiled=True)  49 us
    all_to_all x2, waiting for transfers between devices, fetch_pieces(): lax.all_to_all(outgoing, 'op', split_axis=1, concat_axis=1, tiled=True)  42.5 us
    another operation x4, other arithmetic, body(): lax.linalg.triangular_solve(factor, full_image, left_side=False, lower=Tr...  41.5 us
    all_gather x2, blocking collectives, fetch_pieces(): everyone = lax.all_gather(own_slice, 'sec', axis=0, tiled=True)  16 us
    another operation x7, matrix products, body(): lax.linalg.triangular_solve(factor, full_image, left_side=False, lower=Tr...  15 us
    another operation x12, local copies, waits for them, and re-layouts  14.3 us
  transfers between devices with their start and end apart: 4, of which 4 were waited for; matrix products, arithmetic and copies ran while one was open for 1% of the time, Pallas kernels for 0%

commit v1 on v0

v1 whole, which is shorter than its diff:
```python
import functools

import jax
import jax.numpy as jnp
from jax import lax
from jax.experimental import pallas as pl
from jax.experimental.pallas import tpu as pltpu
from jax.sharding import PartitionSpec as P

LANES = 128
ROWS = 8
HIGHEST = lax.Precision.HIGHEST


def dot_ta(a, b):
    return lax.dot_general(
        a, b, (((0,), (0,)), ((), ())), precision=HIGHEST, preferred_element_type=jnp.float32
    )


def dot(a, b):
    return jnp.dot(a, b, precision=HIGHEST, preferred_element_type=jnp.float32)


def eliminate_tile(tile):
    count = LANES // ROWS
    row = lax.broadcasted_iota(jnp.int32, (ROWS, LANES), 0)
    lane = lax.broadcasted_iota(jnp.int32, (ROWS, LANES), 1)
    left = [tile[ROWS * q : ROWS * (q + 1), :] for q in range(count)]
    right = [jnp.where(lane == row + ROWS * q, 1.0, 0.0).astype(jnp.float32) for q in range(count)]
    for p in range(count):
        upper, lower = left[p], right[p]
        columns = [
            jnp.broadcast_to(upper[:, ROWS * p + j : ROWS * p + j + 1], (ROWS, LANES))
            for j in range(ROWS)
        ]
        for j in range(ROWS):
            scale = lax.rsqrt(jnp.broadcast_to(columns[j][j : j + 1, :], (ROWS, LANES)))
            factor = jnp.where(row > j, columns[j] * scale, 0.0)
            for k in range(j + 1, ROWS):
                own = jnp.broadcast_to(columns[k][j : j + 1, :], (ROWS, LANES)) * scale
                columns[k] = columns[k] - factor * own
            own_upper = jnp.broadcast_to(upper[j : j + 1, :], (ROWS, LANES)) * scale
            own_lower = jnp.broadcast_to(lower[j : j + 1, :], (ROWS, LANES)) * scale
            upper = jnp.where(row == j, own_upper, upper - factor * own_upper)
            lower = jnp.where(row == j, own_lower, lower - factor * own_lower)
        right[p] = lower
        if p + 1 < count:
            change = dot_ta(upper, jnp.concatenate([upper, lower], axis=1))
            for q in range(p + 1, count):
                part = change[ROWS * q : ROWS * (q + 1), :]
                left[q] = left[q] - part[:, :LANES]
                right[q] = right[q] - part[:, LANES:]
    return jnp.concatenate(right, axis=0)


def inverse_factor_kernel(matrix_ref, out_ref, work):
    size = matrix_ref.shape[0]
    blocks = size // LANES
    work[:, :size] = matrix_ref[...]
    work[:, size:] = (
        lax.broadcasted_iota(jnp.int32, (size, size), 0)
        == lax.broadcasted_iota(jnp.int32, (size, size), 1)
    ).astype(jnp.float32)

    def step(b, carry):
        rows = pl.ds(pl.multiple_of(b * LANES, LANES), LANES)
        inverse = eliminate_tile(work[rows, rows])
        panel = dot(inverse, work[rows, :])
        work[rows, :] = panel
        out_ref[rows, :] = panel[:, size:]

        def update(i, inner):
            below = pl.ds(pl.multiple_of(i * LANES, LANES), LANES)
            work[below, :] = work[below, :] - dot_ta(work[rows, below], work[rows, :])
            return inner

        lax.fori_loop(b + 1, blocks, update, 0)
        return carry

    lax.fori_loop(0, blocks, step, 0)


def inverse_factor(matrix):
    size = matrix.shape[0]
    return pl.pallas_call(
        inverse_factor_kernel,
        out_shape=jax.ShapeDtypeStruct((size, size), jnp.float32),
        in_specs=[pl.BlockSpec(memory_space=pltpu.VMEM)],
        out_specs=pl.BlockSpec(memory_space=pltpu.VMEM),
        scratch_shapes=[pltpu.VMEM((size, 2 * size), jnp.float32)],
        compiler_params=pltpu.CompilerParams(vmem_limit_bytes=24 * 1024 * 1024),
        cost_estimate=pl.CostEstimate(flops=2 * size**3, bytes_accessed=8 * size * size, transcendentals=size),
        name="inverse_factor",
    )(matrix)


def source_sectors(target_map):
    sectors = jnp.arange(target_map.shape[1], dtype=jnp.int32)
    matches = target_map[:, :, None] == sectors[None, None, :]
    return jnp.sum(jnp.where(matches, sectors[None, :, None], 0), axis=1)


def fetch_pieces(own_slice, wanted_all):
    everyone = lax.all_gather(own_slice, "sec", axis=0, tiled=True)
    outgoing = jnp.take(everyone, wanted_all, axis=0)
    incoming = lax.all_to_all(outgoing, "op", split_axis=1, concat_axis=1, tiled=True)
    return incoming.reshape(
        incoming.shape[0], incoming.shape[1] * incoming.shape[2], incoming.shape[3]
    )


def body(
    wavefunction,
    op_blocks,
    basis_guess,
    sector_sizes,
    kept_counts,
    target_map,
    noise_numerator,
    noise_denominator,
):
    state_count = wavefunction.shape[2]
    kept_width = basis_guess.shape[2]
    tile_rows = state_count // lax.axis_size("op")
    sec_index = lax.axis_index("sec")
    op_index = lax.axis_index("op")
    noise_weight = noise_numerator[0].astype(jnp.float32) / noise_denominator[0].astype(jnp.float32)
    sources = source_sectors(target_map)
    wanted_all = lax.dynamic_index_in_dim(sources, sec_index, 1, keepdims=False)[None, :]
    wanted = lax.dynamic_index_in_dim(wanted_all[0], op_index, 0, keepdims=False)
    states = jnp.arange(state_count, dtype=jnp.int32)
    own_size = lax.dynamic_index_in_dim(sector_sizes, sec_index, 0, keepdims=False)
    source_size = lax.dynamic_index_in_dim(sector_sizes, wanted, 0, keepdims=False)
    own_count = lax.dynamic_index_in_dim(kept_counts, sec_index, 0, keepdims=False)
    own_kept = jnp.arange(kept_width, dtype=jnp.int32) < own_count
    zero_half = jnp.zeros((), jnp.bfloat16)
    own_rows = jnp.where((states < own_size)[None, :], wavefunction[0], zero_half)
    moved = fetch_pieces(wavefunction, wanted_all)[0]
    moved = jnp.where((states < source_size)[None, :], moved, zero_half)
    blocks = op_blocks[0, 0]
    perturbed = jnp.dot(moved, blocks, preferred_element_type=jnp.float32).astype(jnp.bfloat16)
    guess = jnp.where((states < own_size)[:, None], basis_guess[0], zero_half)
    perturbed_guess = noise_weight * jnp.dot(perturbed, guess, preferred_element_type=jnp.float32)
    own_guess = jnp.dot(own_rows, guess, preferred_element_type=jnp.float32)
    part = lax.dot_general(
        jnp.concatenate([perturbed, own_rows], axis=0).astype(jnp.float32),
        jnp.concatenate([perturbed_guess, own_guess], axis=0),
        (((0,), (0,)), ((), ())),
        precision=HIGHEST,
    )
    part = jnp.where((states < own_size)[:, None] & own_kept[None, :], part, jnp.float32(0.0))
    tile = lax.psum_scatter(part, "op", scatter_dimension=0, tiled=True)
    full_image = lax.all_gather(tile, "op", axis=0, tiled=True)
    padding = jnp.where(own_kept, jnp.float32(0.0), jnp.float32(1.0))
    correlation = dot_ta(full_image, full_image) + padding[:, None] * jnp.eye(
        kept_width, dtype=jnp.float32
    )
    inverse = inverse_factor(correlation)
    new_basis = lax.dot_general(
        full_image, inverse, (((1,), (1,)), ((), ())), precision=HIGHEST
    )
    kept_tile = (
        lax.dynamic_slice_in_dim(new_basis, op_index * tile_rows, tile_rows, 0)
        * float(state_count) ** 0.5
    )
    basis_half = new_basis.astype(jnp.bfloat16)
    mapped = jnp.dot(blocks, basis_half, preferred_element_type=jnp.float32).astype(jnp.bfloat16)
    own_tile = lax.dynamic_slice_in_dim(basis_half, op_index * tile_rows, tile_rows, 0)
    source_basis = fetch_pieces(own_tile[None], wanted_all)[0]
    rotated = lax.dot_general(
        source_basis, mapped, (((0,), (0,)), ((), ())), preferred_element_type=jnp.float32
    )
    return (kept_tile[None], rotated[None, None])


def solution(mesh):
    placed = (
        P("sec", "op", None),
        P("op", "sec", None, None),
        P("sec", None, None),
        P(),
        P(),
        P(),
        P(),
        P(),
    )
    return jax.shard_map(
        body,
        mesh=mesh,
        in_specs=placed,
        out_specs=(P("sec", "op", None), P("op", "sec", None, None)),
        check_vma=False,
    )
```

time: 429 us -> 282 us (0.66); the launches traced: 424 us -> 281 us
  other arithmetic: 128 us -> 10 us
  Pallas kernels: 0 us -> 40.1 us
  matrix products: 43.8 us -> 22.9 us
  local copies, waits for them, and re-layouts: 26.8 us -> 6.12 us
  waiting for transfers between devices: 177 us -> 159 us
  between operations: 22.2 us -> 17.5 us
    another operation x18 -> x0, other arithmetic: 120 us -> none  [the longest x14 78.6 us: body(): factor = jnp.linalg.cholesky(correlation)]
    pallas_call x0 -> x1, Pallas kernels: none -> 40.1 us  [inverse_factor(): pl.pallas_call(inverse_factor_kernel, out_shape=jax.ShapeDtypeStruct((siz...]
    another operation x13 -> x0, matrix products: 20.5 us -> none  [the longest x7 15 us: body(): lax.linalg.triangular_solve(factor, full_image, left_side=False, lower=Tr...]
    reduce_scatter x1, waiting for transfers between devices: 85.2 us -> 67 us  [body(): tile = lax.psum_scatter(part, 'op', scatter_dimension=0, tiled=True)]
    another operation x17 -> x0, local copies, waits for them, and re-layouts: 14.5 us -> none
    dot_general x5 -> x7, matrix products: 23.3 us -> 22.9 us  [the longest x1 5.7 us: dot_ta(): lax.dot_general(a, b, (((0,), (0,)), ((), ())), precision=HIGHEST, prefer...]
  transfers between devices with their start and end apart: 4 -> 4, of which waited for: 4 -> 4; matrix products, arithmetic and copies ran while one was open for 1% -> 3% of each run, Pallas kernels for 0% -> 0%
where the time goes in v1:
time: 282 us; the launch traced here: 281 us
  waiting for transfers between devices  159 us (56%)
  Pallas kernels  40.1 us (14%)
  matrix products  22.9 us (8%)
  between operations  17.5 us (6%)
  blocking collectives  16 us (6%)
  starting transfers between devices  10.1 us (4%)
  other arithmetic  10 us (4%)
  local copies, waits for them, and re-layouts  6.12 us (2%)
    reduce_scatter x1, waiting for transfers between devices, body(): tile = lax.psum_scatter(part, 'op', scatter_dimension=0, tiled=True)  67 us
    all_gather x1, waiting for transfers between devices, body(): full_image = lax.all_gather(tile, 'op', axis=0, tiled=True)  49.7 us
    all_to_all x2, waiting for transfers between devices, fetch_pieces(): lax.all_to_all(outgoing, 'op', split_axis=1, concat_axis=1, tiled=True)  41.8 us
    pallas_call x1, Pallas kernels, inverse_factor(): pl.pallas_call(inverse_factor_kernel, out_shape=jax.ShapeDtypeStruct((siz...  40.1 us
    all_gather x2, blocking collectives, fetch_pieces(): everyone = lax.all_gather(own_slice, 'sec', axis=0, tiled=True)  16 us
    all_to_all x2, starting transfers between devices, fetch_pieces(): lax.all_to_all(outgoing, 'op', split_axis=1, concat_axis=1, tiled=True)  10 us
    dot_general x1, matrix products, dot_ta(): lax.dot_general(a, b, (((0,), (0,)), ((), ())), precision=HIGHEST, prefer...  5.7 us
  transfers between devices with their start and end apart: 4, of which 4 were waited for; matrix products, arithmetic and copies ran while one was open for 3% of the time, Pallas kernels for 0%

profile of v1, /device:TPU:0, one launch (start us, length us, event | category | flops | bytes accessed | tf_op | source)
XLA Modules:
  0.0 281.4 jit_solution(4936540294170623213)
XLA Ops:
  7.2 0.8 select_reduce_fusion
  8.1 8.9 %all_gather.9 = bf16[4,64,1024]{2,1,0:T(8,128)(2,1)S(1)} all-gather(bf16[1,64,1024]{2,1,0:T(8,128)(2,1)} %param.8), channel_id=1, replica_groups=mesh['sec'=4,'op'=8] {'sec'}, dimensions={0}, use_global_device_ids=true | all-gather | bytes 655360 | tf_op jit(solution)/shard_map/all_gather | solution.py:105
  17.0 1.6 gather_fusion
  18.5 2.4 fusion.18
  20.9 5.8 %all-to-all-start = ((bf16[1,8,64,1024]{3,2,0,1:T(8,128)(2,1)}), bf16[1,8,64,1024]{3,2,0,1:T(8,128)(2,1)S(1)}, u32[]{:S(2)}, u32[]{:S(2)}) async-start(bf16[1,8,64,1024]{3,2,0,1:T(8,128)(2,1)} %fusion.18), calls=%async_computation | async-start | bytes 2097152 | tf_op jit(solution)/shard_map/all_to_all | solution.py:107
  26.8 0.6 dynamic_slice.26
  30.0 0.6 dynamic_slice.25
  31.3 0.6 fusion.35
  31.9 0.6 iota_compare_fusion.4
  32.5 0.7 iota_compare_fusion.2
  33.2 0.6 iota_compare_fusion.3
  33.9 2.3 fusion.16
  36.1 16.9 %all-to-all-done = bf16[1,8,64,1024]{3,2,0,1:T(8,128)(2,1)S(1)} async-done(((bf16[1,8,64,1024]{3,2,0,1:T(8,128)(2,1)}), bf16[1,8,64,1024]{3,2,0,1:T(8,128)(2,1)S(1)}, u32[]{:S(2)}, u32[]{:S(2)}) %all-to-all-start) | async-done | bytes 1048608 | tf_op jit(solution)/shard_map/all_to_all | solution.py:107
  53.0 0.1 broadcast_select_fusion
  53.1 1.3 fusion.4
  54.4 0.8 convolution_multiply_fusion
  55.2 0.1 copy-done.8
  55.3 4.0 %and_select_fusion = f32[1024,512]{1,0:T(8,128)} fusion(bf16[64,1024]{1,0:T(8,128)(2,1)S(1)} %bitcast_select_fusion.4, bf16[512,1024]{1,0:T(8,128)(2,1)S(1)} %fusion.4, f32[64,512]{1,0:T(8,128)S(1)} %copy-done.8, f32[512,512]{1,0:T(8,128)S(1)} %convolution_multiply_fusion, pred[512]{0:T(512)(128)(4,1)S(1)} %iota_compare_fusion.4, ...), kind=kOutput, calls=%fused_computation.6 | convolution fusion | flops 3627581440 | bytes 4457984 | tf_op jit(solution)/shard_map/dot_general | solution.py:146
  59.4 67.0 %reduce-scatter.2.cloned.1.call-done = f32[128,512]{1,0:T(8,128)} async-done(((f32[1024,512]{1,0:T(8,128)}), f32[128,512]{1,0:T(8,128)}) %reduce-scatter.2.cloned.1.call-update) | async-done | bytes 262160 | tf_op jit(solution)/shard_map/reduce_scatter | solution.py:153
  126.4 0.6 broadcast_select_fusion.1
  127.1 49.7 %all-gather.3.cloned.1.call-done = f32[1024,512]{1,0:T(8,128)} async-done(((f32[128,512]{1,0:T(8,128)}), f32[1024,512]{1,0:T(8,128)}) %all-gather.3.cloned.1.call-update) | async-done | bytes 2097168 | tf_op jit(solution)/shard_map/all_gather | solution.py:154
  176.8 5.7 %convolution_add_fusion.matrix_ref = f32[512,512]{1,0:T(8,128)S(1)} fusion(f32[1024,512]{1,0:T(8,128)} %all-gather.3.cloned.1.call-done, f32[512]{0:T(512)S(1)} %broadcast_select_fusion.1), kind=kOutput, calls=%fused_computation.10 | convolution fusion | flops 3222011904 | bytes 3147776 | tf_op jit(solution)/shard_map/dot_general | solution.py:16
  182.5 40.1 %inverse_factor.1 = f32[512,512]{1,0:T(8,128)S(1)} custom-call(f32[512,512]{1,0:T(8,128)S(1)} %convolution_add_fusion.matrix_ref), custom_call_target="tpu_custom_call" | custom-call | flops 268435456 | bytes 2097152 | tf_op jit(solution)/shard_map/inverse_factor/pallas_call | solution.py:86
  222.7 4.8 %fusion.36 = (bf16[1024,512]{1,0:T(8,128)(2,1)S(1)}, f32[1024,512]{1,0:T(8,128)}) fusion(f32[1024,512]{1,0:T(8,128)S(1)} %copy-done.1, f32[512,512]{1,0:T(8,128)S(1)} %inverse_factor.1), kind=kOutput, calls=%fused_computation.55 | convolution fusion | flops 3221749760 | bytes 6291456 | tf_op jit(solution)/shard_map/dot_general | solution.py:160
  227.5 1.0 copy-done.2
  228.5 7.1 %all-gather = bf16[512,512]{1,0:T(8,128)(2,1)S(1)} all-gather(bf16[128,512]{1,0:T(8,128)(2,1)S(1)} %constant_dynamic-slice_fusion.1), channel_id=2, replica_groups=mesh['sec'=4,'op'=8] {'sec'}, dimensions={0}, use_global_device_ids=true | all-gather | bytes 655360 | tf_op jit(solution)/shard_map/all_gather | solution.py:105
  235.7 1.6 gather_fusion.1
  237.2 2.4 bitcast_select_fusion
  239.7 4.2 %all-to-all-start.1 = ((bf16[1,8,128,512]{3,2,0,1:T(8,128)(2,1)}), bf16[1,8,128,512]{3,2,0,1:T(8,128)(2,1)}, u32[]{:S(2)}, u32[]{:S(2)}) async-start(bf16[1,8,128,512]{3,2,0,1:T(8,128)(2,1)} %bitcast_select_fusion), calls=%async_computation.2 | async-start | bytes 2097152 | tf_op jit(solution)/shard_map/all_to_all | solution.py:107
  243.9 1.7 multiply_bitcast_fusion
  245.6 24.9 %all-to-all-done.1 = bf16[1,8,128,512]{3,2,0,1:T(8,128)(2,1)} async-done(((bf16[1,8,128,512]{3,2,0,1:T(8,128)(2,1)}), bf16[1,8,128,512]{3,2,0,1:T(8,128)(2,1)}, u32[]{:S(2)}, u32[]{:S(2)}) %all-to-all-start.1) | async-done | bytes 1048608 | tf_op jit(solution)/shard_map/all_to_all | solution.py:107
  270.5 4.0 %convolution_bitcast_fusion = f32[1,1,512,512]{3,2,1,0:T(8,128)} fusion(bf16[1024,512]{1,0:T(8,128)(2,1)} %bitcast.19, bf16[1024,512]{1,0:T(8,128)(2,1)S(1)} %copy-done.3, bf16[1,1,1024,1024]{3,2,1,0:T(8,128)(2,1)S(1)} %copy-done), kind=kOutput, calls=%fused_computation.9 | convolution fusion | flops 1611137024 | bytes 5242880 | tf_op jit(solution)/shard_map/dot_general | solution.py:171
  (25 shorter events, 0.2 us)
Async XLA Ops:
  7.2 45.9 %copy-start = (bf16[1,1,1024,1024]{3,2,1,0:T(8,128)(2,1)S(1)}, bf16[1,1,1024,1024]{3,2,1,0:T(8,128)(2,1)}, u32[]{:S(2)}) copy-start(bf16[1,1,1024,1024]{3,2,1,0:T(8,128)(2,1)} %param.9) | copy-start | bytes 6291460
  18.5 11.4 %copy-start.7 = (s32[4]{0:T(128)S(1)}, s32[4]{0:T(128)}, u32[]{:S(2)}) copy-start(s32[4]{0:T(128)} %param.12) | copy-start | bytes 52
  18.5 12.7 %copy-start.5 = (s32[4]{0:T(128)S(1)}, s32[4]{0:T(128)}, u32[]{:S(2)}) copy-start(s32[4]{0:T(128)} %param.11) | copy-start | bytes 52
  18.5 15.3 %copy-start.4 = (bf16[1,64,1024]{2,1,0:T(8,128)(2,1)S(1)}, bf16[1,64,1024]{2,1,0:T(8,128)(2,1)}, u32[]{:S(2)}) copy-start(bf16[1,64,1024]{2,1,0:T(8,128)(2,1)} %param.8) | copy-start | bytes 393220
  20.9 32.1 %all-to-all-start = ((bf16[1,8,64,1024]{3,2,0,1:T(8,128)(2,1)}), bf16[1,8,64,1024]{3,2,0,1:T(8,128)(2,1)S(1)}, u32[]{:S(2)}, u32[]{:S(2)}) async-start(bf16[1,8,64,1024]{3,2,0,1:T(8,128)(2,1)} %fusion.18), calls=%async_computation | async-start | bytes 2097152 | tf_op jit(solution)/shard_map/all_to_all | solution.py:107
  26.7 99.7 %reduce-scatter.2.cloned.1.call-start = ((), (), s32[]{:S(2)}) async-start(), calls=%async_computation.3 | async-start | bytes 2359296 | tf_op jit(solution)/shard_map/reduce_scatter | solution.py:153
  53.1 1.3 copy-start.6
  54.4 0.9 copy-start.8
  59.4 117.4 %all-gather.3.cloned.1.call-start = ((), (), s32[]{:S(2)}) async-start(), calls=%async_computation.4 | async-start | bytes 2359296 | tf_op jit(solution)/shard_map/all_gather | solution.py:154
  182.5 40.2 %copy-start.1 = (f32[1024,512]{1,0:T(8,128)S(1)}, f32[1024,512]{1,0:T(8,128)}, u32[]{:S(2)}) copy-start(f32[1024,512]{1,0:T(8,128)} %all-gather.3.cloned.1.call-done) | copy-start | bytes 6291460
  227.5 1.0 copy-start.2
  237.2 33.2 %copy-start.3 = (bf16[1024,512]{1,0:T(8,128)(2,1)S(1)}, bf16[1024,512]{1,0:T(8,128)(2,1)}, u32[]{:S(2)}) copy-start(bf16[1024,512]{1,0:T(8,128)(2,1)} %copy-done.2) | copy-start | bytes 3145732
  239.7 30.8 %all-to-all-start.1 = ((bf16[1,8,128,512]{3,2,0,1:T(8,128)(2,1)}), bf16[1,8,128,512]{3,2,0,1:T(8,128)(2,1)}, u32[]{:S(2)}, u32[]{:S(2)}) async-start(bf16[1,8,128,512]{3,2,0,1:T(8,128)(2,1)} %bitcast_select_fusion), calls=%async_computation.2 | async-start | bytes 2097152 | tf_op jit(solution)/shard_map/all_to_all | solution.py:107
Sparse Core Ops, SparseCore 0:
  59.5 66.8 reduce-scatter.1
  128.5 48.2 all-gather.2
